TPU v7x, 32 devices: a whole 2x2x4 slice. The times are simulated.
32 devices in a mesh: band: 8 (over z, y), dir: 4 (over x, core).
Axes of the slice: x: 2, y: 2, z: 4, core: 2. Of those that a mesh axis runs over, the one named last changes fastest.
Arguments:
- visibilities: float32 [8, 2, 2, 2, 16, 512], P('band'), may hold values from -6 to 6
- coherencies: float32 [8, 16, 2, 2, 2, 16, 512], P('band', 'dir'), may hold values from -1.2 to 1.2
- jones_start: float32 [8, 16, 2, 2, 2, 1024], P('band', 'dir'), may hold values from -3.6 to 3.6
- dual_start: float32 [8, 16, 2, 2, 2, 1024], P('band', 'dir'), may hold values from -6 to 6
- consensus_start: float32 [8, 16, 2, 2, 2, 1024], P(None, 'dir'), may hold values from -1.8 to 1.8
- freq_basis: float32 [8, 8], P('band'), may hold values from -1 to 1
- baseline_station_pairs: int32 [2, 512], replicated, may hold values from 0 to 1023
Outputs:
- jones_final: float32 [8, 16, 2, 2, 2, 1024], P('band', 'dir')
- dual_final: float32 [8, 16, 2, 2, 2, 1024], P('band', 'dir')
- consensus_coeffs: float32 [8, 16, 2, 2, 2, 1024], P(None, 'dir')
All inputs are finite; a program needn't handle non-finite values.
Results may differ from a plain program's by a relative error of at most 0.0003.
Values sent between devices are 32-bit elements; how exact they have to be, the bound alone decides.
No kernel may reach another device: no remote copies, remote signals or barrier semaphores. Data moves between devices by JAX's collectives and lax.ppermute only.
A program may use at most 128 MiB of HBM per device.

v0:
```python
import jax
import jax.numpy as jnp
from jax import lax
from jax.sharding import PartitionSpec as P

ITERS = 3
RHO = 5.0
RIDGE = 0.25


def small_mul(left, right):
    return left[:, 0:1] * right[0:1] + left[:, 1:2] * right[1:2]


def complex_mul(left, right):
    real_part = small_mul(left[0], right[0]) - small_mul(left[1], right[1])
    imag_part = small_mul(left[0], right[1]) + small_mul(left[1], right[0])
    return jnp.stack([real_part, imag_part])


def hermitian(value):
    return jnp.stack([jnp.swapaxes(value[0], 0, 1), -jnp.swapaxes(value[1], 0, 1)])


def solve_right(numer, matrix):
    adjugate = jnp.stack(
        [
            jnp.stack([matrix[:, 1, 1], -matrix[:, 0, 1]], axis=1),
            jnp.stack([-matrix[:, 1, 0], matrix[:, 0, 0]], axis=1),
        ],
        axis=1,
    )
    det_real = (
        matrix[0, 0, 0] * matrix[0, 1, 1]
        - matrix[1, 0, 0] * matrix[1, 1, 1]
        - (matrix[0, 0, 1] * matrix[0, 1, 0] - matrix[1, 0, 1] * matrix[1, 1, 0])
    )
    det_imag = (
        matrix[0, 0, 0] * matrix[1, 1, 1]
        + matrix[1, 0, 0] * matrix[0, 1, 1]
        - (matrix[0, 0, 1] * matrix[1, 1, 0] + matrix[1, 0, 1] * matrix[0, 1, 0])
    )
    product = complex_mul(numer, adjugate)
    divisor = det_real * det_real + det_imag * det_imag
    real_part = (product[0] * det_real + product[1] * det_imag) / divisor
    imag_part = (product[1] * det_real - product[0] * det_imag) / divisor
    return jnp.stack([real_part, imag_part])


def predict(jones_k, coher_k, first, second):
    jones_first = jnp.take(jones_k, first, axis=-1)[..., None, :]
    jones_second = jnp.take(jones_k, second, axis=-1)[..., None, :]
    return complex_mul(complex_mul(jones_first, coher_k), hermitian(jones_second))


def baseline_terms(target, jones_k, coher_k, first, second):
    jones_first = jnp.take(jones_k, first, axis=-1)[..., None, :]
    jones_second = jnp.take(jones_k, second, axis=-1)[..., None, :]
    along_term = complex_mul(coher_k, hermitian(jones_second))
    back_term = hermitian(complex_mul(jones_first, coher_k))
    flipped = hermitian(target)
    right_first = jnp.sum(complex_mul(target, hermitian(along_term)), axis=-2)
    normal_first = jnp.sum(complex_mul(along_term, hermitian(along_term)), axis=-2)
    right_second = jnp.sum(complex_mul(flipped, hermitian(back_term)), axis=-2)
    normal_second = jnp.sum(complex_mul(back_term, hermitian(back_term)), axis=-2)
    first_part = jnp.concatenate([right_first.reshape(8, -1), normal_first.reshape(8, -1)], axis=0)
    second_part = jnp.concatenate(
        [right_second.reshape(8, -1), normal_second.reshape(8, -1)], axis=0
    )
    return jnp.concatenate([first_part, second_part], axis=1)


def update_one(right_sum, normal_sum, consensus, dual):
    identity = jnp.stack([jnp.eye(2, dtype=jnp.float32), jnp.zeros((2, 2), jnp.float32)])[..., None]
    matrix = normal_sum + RHO * identity
    return solve_right(right_sum + RHO * consensus - dual, matrix)


def apply_inverse(scale_factor, sums):
    flat = sums.reshape(sums.shape[0], -1)
    return jax.scipy.linalg.cho_solve((scale_factor, True), flat).reshape(sums.shape)


def local(
    visibilities,
    coherencies,
    jones_start,
    dual_start,
    consensus_start,
    freq_basis,
    baseline_station_pairs,
):
    coefficient_row = freq_basis[0]
    terms = coefficient_row.shape[0]
    outer = coefficient_row[:, None] * coefficient_row[None, :]
    gram = lax.psum(outer, "band") + RIDGE * lax.axis_size("band") * jnp.eye(
        terms, dtype=jnp.float32
    )
    scale_factor = jnp.linalg.cholesky(gram)
    first = baseline_station_pairs[0]
    second = baseline_station_pairs[1]
    stations = jones_start.shape[-1]
    station_ids = jnp.arange(stations, dtype=jnp.int32)
    onehots = (jnp.concatenate([first, second])[:, None] == station_ids[None, :]).astype(
        jnp.float32
    )
    vis_band = visibilities[0]
    coher_band = coherencies[0]
    jones = jones_start[0]
    dual = dual_start[0]
    dirs = jones.shape[0]
    coeffs = consensus_start
    consensus = jnp.tensordot(coefficient_row, coeffs, axes=(0, 0), precision=lax.Precision.HIGHEST)
    for turn_index in range(ITERS):
        model_terms = jax.vmap(predict, (0, 0, None, None))(jones, coher_band, first, second)
        model_total = lax.psum(jnp.sum(model_terms, axis=0), "dir")
        residual = vis_band - model_total
        normal_terms = jax.vmap(baseline_terms, (0, 0, 0, None, None))(
            residual[None] + model_terms, jones, coher_band, first, second
        )
        stacked = normal_terms.reshape(dirs * 16, -1)
        segment = jnp.dot(stacked, onehots, precision=lax.Precision.HIGHEST)
        segment = segment.reshape((dirs, 2, 2, 2, 2, stations))
        jones = jax.vmap(update_one)(segment[:, 0], segment[:, 1], consensus, dual)
        local_terms = coefficient_row.reshape((terms, 1, 1, 1, 1, 1)) * (jones + dual / RHO)[None]
        coeff_sums = lax.psum(local_terms, "band")
        coeffs = apply_inverse(scale_factor, coeff_sums)
        consensus = jnp.tensordot(
            coefficient_row, coeffs, axes=(0, 0), precision=lax.Precision.HIGHEST
        )
        dual = dual + RHO * (jones - consensus)
    return (jones[None], dual[None], coeffs)


def solution(mesh):
    in_specs = (
        P("band", None, None, None, None, None),
        P("band", "dir", None, None, None, None, None),
        P("band", "dir", None, None, None, None),
        P("band", "dir", None, None, None, None),
        P(None, "dir", None, None, None, None),
        P("band", None),
        P(),
    )
    out_specs = (
        P("band", "dir", None, None, None, None),
        P("band", "dir", None, None, None, None),
        P(None, "dir", None, None, None, None),
    )
    return jax.shard_map(local, mesh=mesh, in_specs=in_specs, out_specs=out_specs, check_vma=False)
```

profile of v0, /device:TPU:0, one launch (start us, length us, event | category | flops | bytes accessed | tf_op | source)
XLA Modules:
  0.0 537.6 jit_solution(1846712404722757130)
XLA Ops:
  8.1 2.3 slice_bitcast_fusion.13
  10.4 4.4 copy.255
  14.8 7.1 %gather_fusion = f32[512,4,2,2,2]{1,4,3,2,0:T(2,128)} fusion(f32[4,2,2,2,1024]{0,3,4,2,1:T(2,128)} %bitcast.712, s32[1024]{0:T(1024)S(1)} %pad_clamp_fusion.1), kind=kCustom, calls=%fused_computation.clone | custom fusion | bytes 133120 | tf_op jit(solution)/shard_map/vmap(jit(_take))/gather | solution.py:51
  22.0 3.1 select_bitcast_fusion.5
  28.2 7.2 %gather_fusion.1 = f32[512,4,2,2,2]{1,4,3,2,0:T(2,128)} fusion(f32[4,2,2,2,1024]{0,3,4,2,1:T(2,128)} %bitcast.713, s32[1024]{0:T(1024)S(1)} %pad_clamp_fusion), kind=kCustom, calls=%fused_computation.1.clone | custom fusion | bytes 133120 | tf_op jit(solution)/shard_map/vmap(jit(_take))/gather | solution.py:52
  35.4 3.4 select_bitcast_fusion.4
  39.6 2.6 fusion.90
  64.8 23.1 %psum.51 = f32[8,8]{0,1:T(8,128)S(1)} all-reduce(f32[8,8]{0,1:T(8,128)S(1)} %broadcast_multiply_fusion.3), channel_id=1, replica_groups=mesh['band'=8,'dir'=4] {'band'}, use_global_device_ids=true, to_apply=%region_12.14 | all-reduce | flops 64 | bytes 512 | tf_op jit(solution)/shard_map/psum | solution.py:96
  101.2 4.6 copy.288
  105.8 7.1 %gather_fusion.2 = f32[512,4,2,2,2]{1,4,3,2,0:T(2,128)} fusion(f32[4,2,2,2,1024]{0,3,4,2,1:T(2,128)} %copy.288, s32[1024]{0:T(1024)S(1)} %pad_clamp_fusion.1), kind=kCustom, calls=%fused_computation.2.clone | custom fusion | bytes 133120 | tf_op jit(solution)/shard_map/vmap(jit(_take))/gather | solution.py:51
  112.9 7.1 %gather_fusion.3 = f32[512,4,2,2,2]{1,4,3,2,0:T(2,128)} fusion(f32[4,2,2,2,1024]{0,3,4,2,1:T(2,128)} %copy.288, s32[1024]{0:T(1024)S(1)} %copy-done.112), kind=kCustom, calls=%fused_computation.3.clone | custom fusion | bytes 133120 | tf_op jit(solution)/shard_map/vmap(jit(_take))/gather | solution.py:52
  120.1 3.0 select_bitcast_fusion.3
  148.4 2.5 fusion.86
  170.6 18.1 %all-reduce.10.cloned.1.call-done = f32[2,2,2,16,512]{4,3,2,1,0:T(8,128)} async-done(((f32[2,2,2,16,512]{4,3,2,1,0:T(8,128)}), f32[2,2,2,16,512]{4,3,2,1,0:T(8,128)}) %all-reduce.10.cloned.1.call-update) | async-done | bytes 262160 | tf_op jit(solution)/shard_map/psum | solution.py:116
  196.1 2.4 fusion.3
  198.6 72.6 %all-reduce.12.cloned.1.call-done = f32[8,32768]{1,0:T(8,128)} async-done(((f32[8,32768]{1,0:T(8,128)}), f32[8,32768]{1,0:T(8,128)}) %all-reduce.12.cloned.1.call-update) | async-done | bytes 1048592 | tf_op jit(solution)/shard_map/psum | solution.py:126
  271.1 2.3 fusion.68
  276.8 4.6 copy.327
  281.4 7.1 %gather_fusion.4 = f32[512,4,2,2,2]{1,4,3,2,0:T(2,128)} fusion(f32[4,2,2,2,1024]{0,3,4,2,1:T(2,128)} %copy.327, s32[1024]{0:T(1024)S(1)} %pad_clamp_fusion.1), kind=kCustom, calls=%fused_computation.4.clone | custom fusion | bytes 133120 | tf_op jit(solution)/shard_map/vmap(jit(_take))/gather | solution.py:51
  288.5 7.1 %gather_fusion.5 = f32[512,4,2,2,2]{1,4,3,2,0:T(2,128)} fusion(f32[4,2,2,2,1024]{0,3,4,2,1:T(2,128)} %copy.327, s32[1024]{0:T(1024)S(1)} %copy-done.113), kind=kCustom, calls=%fused_computation.5.clone | custom fusion | bytes 133120 | tf_op jit(solution)/shard_map/vmap(jit(_take))/gather | solution.py:52
  295.6 3.0 select_bitcast_fusion.1
  332.9 22.8 %all-reduce.14.cloned.1.call-done = f32[2,2,2,16,512]{4,3,2,1,0:T(8,128)} async-done(((f32[2,2,2,16,512]{4,3,2,1,0:T(8,128)}), f32[2,2,2,16,512]{4,3,2,1,0:T(8,128)}) %all-reduce.14.cloned.1.call-update) | async-done | bytes 262160 | tf_op jit(solution)/shard_map/psum | solution.py:116
  363.6 74.3 %all-reduce.16.cloned.1.call-done = f32[8,32768]{1,0:T(8,128)} async-done(((f32[8,32768]{1,0:T(8,128)}), f32[8,32768]{1,0:T(8,128)}) %all-reduce.16.cloned.1.call-update) | async-done | bytes 1048592 | tf_op jit(solution)/shard_map/psum | solution.py:126
  446.2 77.2 %all-reduce.18.cloned.1.call-done = f32[8,32768]{1,0:T(8,128)} async-done(((f32[8,32768]{1,0:T(8,128)}), f32[8,32768]{1,0:T(8,128)}) %all-reduce.18.cloned.1.call-update) | async-done | bytes 1048592 | tf_op jit(solution)/shard_map/psum | solution.py:126
  (508 shorter events, 152.0 us)
Async XLA Ops:
  7.2 55.4 %copy-start = (f32[8,4,2,2,2,1024]{5,4,3,2,1,0:T(2,128)S(1)}, f32[8,4,2,2,2,1024]{5,4,3,2,1,0:T(2,128)}, u32[]{:S(2)}) copy-start(f32[8,4,2,2,2,1024]{5,4,3,2,1,0:T(2,128)} %param.15) | copy-start | bytes 3145732
  7.2 84.3 %all-reduce.8.cloned.1.call-start = ((), (), s32[]{:S(2)}) async-start(), calls=%async_computation | async-start | bytes 524288 | tf_op jit(solution)/shard_map/psum | solution.py:116
  8.1 13.9 %copy-start.117 = (pred[512]{0:T(512)(128)(4,1)}, pred[512]{0:T(512)(128)(4,1)S(1)}, u32[]{:S(2)}) copy-start(pred[512]{0:T(512)(128)(4,1)S(1)} %compare_and_fusion) | copy-start | bytes 1540
  8.1 27.3 %copy-start.114 = (pred[512]{0:T(512)(128)(4,1)}, pred[512]{0:T(512)(128)(4,1)S(1)}, u32[]{:S(2)}) copy-start(pred[512]{0:T(512)(128)(4,1)S(1)} %compare_and_fusion.1) | copy-start | bytes 1540
  28.2 10.5 %copy-start.111 = (s32[1024]{0:T(1024)}, s32[1024]{0:T(1024)S(1)}, u32[]{:S(2)}) copy-start(s32[1024]{0:T(1024)S(1)} %pad_clamp_fusion) | copy-start | bytes 12292
  48.1 140.6 %all-reduce.10.cloned.1.call-start = ((), (), s32[]{:S(2)}) async-start(), calls=%async_computation.1 | async-start | bytes 524288 | tf_op jit(solution)/shard_map/psum | solution.py:116
  60.0 31.6 %copy-start.12 = (f32[1,2,2,2,16,512]{5,4,3,2,1,0:T(8,128)S(1)}, f32[1,2,2,2,16,512]{5,4,3,2,1,0:T(8,128)}, u32[]{:S(2)}) copy-start(f32[1,2,2,2,16,512]{5,4,3,2,1,0:T(8,128)} %param.11) | copy-start | bytes 786436
  101.1 4.7 copy-start.89
  101.2 4.7 copy-start.92
  101.2 11.7 %copy-start.112 = (s32[1024]{0:T(1024)S(1)}, s32[1024]{0:T(1024)}, u32[]{:S(2)}) copy-start(s32[1024]{0:T(1024)} %copy-done.111) | copy-start | bytes 12292
  101.2 18.9 %copy-start.118 = (pred[512]{0:T(512)(128)(4,1)S(1)}, pred[512]{0:T(512)(128)(4,1)}, u32[]{:S(2)}) copy-start(pred[512]{0:T(512)(128)(4,1)} %copy-done.117) | copy-start | bytes 1540
  158.1 5.8 %copy-start.4 = (f32[1,4,2,2,16,512]{5,4,3,2,1,0:T(8,128)}, f32[1,4,2,2,16,512]{5,4,3,2,1,0:T(8,128)S(1)}, u32[]{:S(2)}) copy-start(f32[1,4,2,2,16,512]{5,4,3,2,1,0:T(8,128)S(1)} %get-tuple-element.80) | copy-start | bytes 1572868
  158.1 5.8 %copy-start.5 = (f32[1,4,2,2,16,512]{5,4,3,2,1,0:T(8,128)}, f32[1,4,2,2,16,512]{5,4,3,2,1,0:T(8,128)S(1)}, u32[]{:S(2)}) copy-start(f32[1,4,2,2,16,512]{5,4,3,2,1,0:T(8,128)S(1)} %get-tuple-element.81) | copy-start | bytes 1572868
  159.0 112.1 %all-reduce.12.cloned.1.call-start = ((), (), s32[]{:S(2)}) async-start(), calls=%async_computation.2 | async-start | bytes 2097152 | tf_op jit(solution)/shard_map/psum | solution.py:126
  159.1 4.8 copy-start.21
  159.1 5.6 %copy-start.19 = (f32[4,2,2,16,512]{4,3,1,0,2:T(8,128)S(1)}, f32[4,2,2,16,512]{4,3,1,0,2:T(8,128)}, u32[]{:S(2)}) copy-start(f32[4,2,2,16,512]{4,3,1,0,2:T(8,128)} %get-tuple-element.79) | copy-start | bytes 1572868
  170.1 185.6 %all-reduce.14.cloned.1.call-start = ((), (), s32[]{:S(2)}) async-start(), calls=%async_computation.3 | async-start | bytes 524288 | tf_op jit(solution)/shard_map/psum | solution.py:116
  276.7 4.7 copy-start.83
  276.7 4.7 copy-start.86
  276.7 11.7 %copy-start.113 = (s32[1024]{0:T(1024)S(1)}, s32[1024]{0:T(1024)}, u32[]{:S(2)}) copy-start(s32[1024]{0:T(1024)} %copy-done.111) | copy-start | bytes 12292
  276.8 18.9 %copy-start.119 = (pred[512]{0:T(512)(128)(4,1)S(1)}, pred[512]{0:T(512)(128)(4,1)}, u32[]{:S(2)}) copy-start(pred[512]{0:T(512)(128)(4,1)} %copy-done.117) | copy-start | bytes 1540
  323.6 114.3 %all-reduce.16.cloned.1.call-start = ((), (), s32[]{:S(2)}) async-start(), calls=%async_computation.4 | async-start | bytes 2097152 | tf_op jit(solution)/shard_map/psum | solution.py:126
  332.6 190.8 %all-reduce.18.cloned.1.call-start = ((), (), s32[]{:S(2)}) async-start(), calls=%async_computation.5 | async-start | bytes 2097152 | tf_op jit(solution)/shard_map/psum | solution.py:126
  525.7 4.7 copy-start.1
  (105 other events, 223.5 us)
Sparse Core Ops, SparseCore 0:
  48.3 34.9 all-reduce.7
  159.1 29.5 all-reduce.9
  192.8 78.2 all-reduce.11
  323.8 31.8 all-reduce.13
  359.6 78.2 all-reduce.15
  445.6 77.8 all-reduce.17
where the time goes:
time: 548 us; the launch traced here: 538 us
  waiting for transfers between devices  265 us (48%)
  local copies, waits for them, and re-layouts  155 us (28%)
  other arithmetic  56.7 us (10%)
  blocking collectives  23.1 us (4%)
  matrix products  20.7 us (4%)
  between operations  16.6 us (3%)
    psum x3, waiting for transfers between devices, local(): coeff_sums = lax.psum(local_terms, 'band')  224 us
    mul x92, local copies, waits for them, and re-layouts, small_mul(): return left[:, 0:1] * right[0:1] + left[:, 1:2] * right[1:2]  57.9 us
    psum x3, waiting for transfers between devices, local(): model_total = lax.psum(jnp.sum(model_terms, axis=0), 'dir')  40.9 us
    psum x1, blocking collectives, local(): lax.psum(outer, 'band')  23.1 us
    gather x3, local copies, waits for them, and re-layouts, predict(): jones_second = jnp.take(jones_k, second, axis=-1)[..., None, :]  21.4 us
    gather x3, local copies, waits for them, and re-layouts, predict(): jones_first = jnp.take(jones_k, first, axis=-1)[..., None, :]  21.3 us
    slice x10, local copies, waits for them, and re-layouts, small_mul(): return left[:, 0:1] * right[0:1] + left[:, 1:2] * right[1:2]  16.4 us
    unnamed x250, local copies, waits for them, and re-layouts  15.9 us
  transfers between devices with their start and end apart: 6, of which 5 were waited for; matrix products, arithmetic and copies ran while one was open for 10% of the time, Pallas kernels for 0%

commit v1 on v0

--- a/solution.py
+++ b/solution.py
@@ -123,7 +123,11 @@
         segment = segment.reshape((dirs, 2, 2, 2, 2, stations))
         jones = jax.vmap(update_one)(segment[:, 0], segment[:, 1], consensus, dual)
         local_terms = coefficient_row.reshape((terms, 1, 1, 1, 1, 1)) * (jones + dual / RHO)[None]
-        coeff_sums = lax.psum(local_terms, "band")
+        coeff_sums = local_terms
+        for hop in (1, 2, 4):
+            coeff_sums = coeff_sums + lax.ppermute(
+                coeff_sums, "band", [(dev, dev ^ hop) for dev in range(8)]
+            )
         coeffs = apply_inverse(scale_factor, coeff_sums)
         consensus = jnp.tensordot(
             coefficient_row, coeffs, axes=(0, 0), precision=lax.Precision.HIGHEST

time: 548 us -> 564 us (1.029)
  starting transfers between devices: 0.9 us -> 17.3 us
  other arithmetic: 56.7 us -> 69.1 us
  waiting for transfers between devices: 265 us -> 255 us
    psum x3 -> x0, waiting for transfers between devices: 224 us -> none  [local(): coeff_sums = lax.psum(local_terms, 'band')]
    ppermute x0 -> x9, waiting for transfers between devices: none -> 210 us  [local(): lax.ppermute(coeff_sums, 'band', [(dev, dev ^ hop) for dev in range(8)])]
    ppermute x0 -> x9, starting transfers between devices: none -> 17.2 us  [local(): lax.ppermute(coeff_sums, 'band', [(dev, dev ^ hop) for dev in range(8)])]
    add x0 -> x9, other arithmetic: none -> 11.2 us  [local(): coeff_sums + lax.ppermute(coeff_sums, 'band', [(dev, dev ^ hop) for dev i...]
    mul x92, local copies, waits for them, and re-layouts: 57.9 us -> 64.6 us  [small_mul(): return left[:, 0:1] * right[0:1] + left[:, 1:2] * right[1:2]]
    unnamed x250 -> x274, local copies, waits for them, and re-layouts: 15.9 us -> 11.9 us
  transfers between devices with their start and end apart: 6 -> 12, of which waited for: 5 -> 9; matrix products, arithmetic and copies ran while one was open for 10% -> 9% of each run, Pallas kernels for 0% -> 0%
where the time goes in v1:
time: 564 us; the launch traced here: 554 us
  waiting for transfers between devices  255 us (45%)
  local copies, waits for them, and re-layouts  155 us (27%)
  other arithmetic  69.1 us (12%)
  blocking collectives  23.1 us (4%)
  matrix products  17.5 us (3%)
  starting transfers between devices  17.3 us (3%)
  between operations  16.7 us (3%)
    ppermute x9, waiting for transfers between devices, local(): lax.ppermute(coeff_sums, 'band', [(dev, dev ^ hop) for dev in range(8)])  210 us
    mul x92, local copies, waits for them, and re-layouts, small_mul(): return left[:, 0:1] * right[0:1] + left[:, 1:2] * right[1:2]  64.6 us
    psum x3, waiting for transfers between devices, local(): model_total = lax.psum(jnp.sum(model_terms, axis=0), 'dir')  44.8 us
    psum x1, blocking collectives, local(): lax.psum(outer, 'band')  23.1 us
    gather x3, local copies, waits for them, and re-layouts, predict(): jones_second = jnp.take(jones_k, second, axis=-1)[..., None, :]  21.5 us
    gather x3, local copies, waits for them, and re-layouts, predict(): jones_first = jnp.take(jones_k, first, axis=-1)[..., None, :]  21.4 us
    ppermute x9, starting transfers between devices, local(): lax.ppermute(coeff_sums, 'band', [(dev, dev ^ hop) for dev in range(8)])  17.2 us
    slice x10, local copies, waits for them, and re-layouts, small_mul(): return left[:, 0:1] * right[0:1] + left[:, 1:2] * right[1:2]  17.1 us
  transfers between devices with their start and end apart: 12, of which 9 were waited for; matrix products, arithmetic and copies ran while one was open for 9% of the time, Pallas kernels for 0%

profile of v1, /device:TPU:0, one launch (start us, length us, event | category | flops | bytes accessed | tf_op | source)
XLA Modules:
  0.0 554.1 jit_solution(7045922903503104838)
XLA Ops:
  9.4 4.5 copy.255
  13.9 7.2 %gather_fusion = f32[512,4,2,2,2]{1,4,3,2,0:T(2,128)} fusion(f32[4,2,2,2,1024]{0,3,4,2,1:T(2,128)} %bitcast.712, s32[1024]{0:T(1024)S(1)} %pad_clamp_fusion.1), kind=kCustom, calls=%fused_computation.clone | custom fusion | bytes 133120 | tf_op jit(solution)/shard_map/vmap(jit(_take))/gather | solution.py:51
  21.1 3.1 select_bitcast_fusion.5
  30.4 7.2 %gather_fusion.1 = f32[512,4,2,2,2]{1,4,3,2,0:T(2,128)} fusion(f32[4,2,2,2,1024]{0,3,4,2,1:T(2,128)} %bitcast.713, s32[1024]{0:T(1024)S(1)} %pad_clamp_fusion), kind=kCustom, calls=%fused_computation.1.clone | custom fusion | bytes 133120 | tf_op jit(solution)/shard_map/vmap(jit(_take))/gather | solution.py:52
  37.5 3.2 select_bitcast_fusion.4
  66.6 23.1 %psum.30 = f32[8,8]{0,1:T(8,128)S(1)} all-reduce(f32[8,8]{0,1:T(8,128)S(1)} %broadcast_multiply_fusion.3), channel_id=1, replica_groups=mesh['band'=8,'dir'=4] {'band'}, use_global_device_ids=true, to_apply=%region_12.14 | all-reduce | flops 64 | bytes 512 | tf_op jit(solution)/shard_map/psum | solution.py:96
  103.1 4.9 copy.288
  107.9 7.1 %gather_fusion.2 = f32[512,4,2,2,2]{1,4,3,2,0:T(2,128)} fusion(f32[4,2,2,2,1024]{0,3,4,2,1:T(2,128)} %copy.288, s32[1024]{0:T(1024)S(1)} %pad_clamp_fusion.1), kind=kCustom, calls=%fused_computation.2.clone | custom fusion | bytes 133120 | tf_op jit(solution)/shard_map/vmap(jit(_take))/gather | solution.py:51
  115.0 7.2 %gather_fusion.3 = f32[512,4,2,2,2]{1,4,3,2,0:T(2,128)} fusion(f32[4,2,2,2,1024]{0,3,4,2,1:T(2,128)} %copy.288, s32[1024]{0:T(1024)S(1)} %copy-done.124), kind=kCustom, calls=%fused_computation.3.clone | custom fusion | bytes 133120 | tf_op jit(solution)/shard_map/vmap(jit(_take))/gather | solution.py:52
  122.2 3.0 select_bitcast_fusion.3
  170.1 20.6 %all-reduce.7.cloned.1.call-done = f32[2,2,2,16,512]{4,3,2,1,0:T(8,128)} async-done(((f32[2,2,2,16,512]{4,3,2,1,0:T(8,128)}), f32[2,2,2,16,512]{4,3,2,1,0:T(8,128)}) %all-reduce.7.cloned.1.call-update) | async-done | bytes 262160 | tf_op jit(solution)/shard_map/psum | solution.py:116
  197.8 21.1 %collective-permute-done.1 = f32[8,4,2,2,2,1024]{5,4,3,2,1,0:T(2,128)S(1)} collective-permute-done((f32[8,4,2,2,2,1024]{5,4,3,2,1,0:T(2,128)S(1)}, f32[8,4,2,2,2,1024]{5,4,3,2,1,0:T(2,128)S(1)}, u32[]{:S(2)}, u32[]{:S(2)}) %collective-permute-start.1) | collective-permute-done | bytes 1048608 | tf_op jit(solution)/shard_map/ppermute | solution.py:128
  228.4 39.2 %collective-permute-done.2 = f32[8,4,2,2,2,1024]{5,4,3,2,1,0:T(2,128)S(1)} collective-permute-done((f32[8,4,2,2,2,1024]{5,4,3,2,1,0:T(2,128)S(1)}, f32[8,4,2,2,2,1024]{5,4,3,2,1,0:T(2,128)S(1)}, u32[]{:S(2)}, u32[]{:S(2)}) %collective-permute-start.2) | collective-permute-done | bytes 1048608 | tf_op jit(solution)/shard_map/ppermute | solution.py:128
  275.7 4.4 copy.327
  280.1 7.1 %gather_fusion.4 = f32[512,4,2,2,2]{1,4,3,2,0:T(2,128)} fusion(f32[4,2,2,2,1024]{0,3,4,2,1:T(2,128)} %copy.327, s32[1024]{0:T(1024)S(1)} %pad_clamp_fusion.1), kind=kCustom, calls=%fused_computation.4.clone | custom fusion | bytes 133120 | tf_op jit(solution)/shard_map/vmap(jit(_take))/gather | solution.py:51
  287.2 7.2 %gather_fusion.5 = f32[512,4,2,2,2]{1,4,3,2,0:T(2,128)} fusion(f32[4,2,2,2,1024]{0,3,4,2,1:T(2,128)} %copy.327, s32[1024]{0:T(1024)S(1)} %copy-done.125), kind=kCustom, calls=%fused_computation.5.clone | custom fusion | bytes 133120 | tf_op jit(solution)/shard_map/vmap(jit(_take))/gather | solution.py:52
  294.4 3.0 select_bitcast_fusion.1
  337.8 24.2 %all-reduce.9.cloned.1.call-done = f32[2,2,2,16,512]{4,3,2,1,0:T(8,128)} async-done(((f32[2,2,2,16,512]{4,3,2,1,0:T(8,128)}), f32[2,2,2,16,512]{4,3,2,1,0:T(8,128)}) %all-reduce.9.cloned.1.call-update) | async-done | bytes 262160 | tf_op jit(solution)/shard_map/psum | solution.py:116
  366.5 21.3 %collective-permute-done.4 = f32[8,4,2,2,2,1024]{5,4,3,2,1,0:T(2,128)S(1)} collective-permute-done((f32[8,4,2,2,2,1024]{5,4,3,2,1,0:T(2,128)S(1)}, f32[8,4,2,2,2,1024]{5,4,3,2,1,0:T(2,128)S(1)}, u32[]{:S(2)}, u32[]{:S(2)}) %collective-permute-start.4) | collective-permute-done | bytes 1048608 | tf_op jit(solution)/shard_map/ppermute | solution.py:128
  395.4 40.0 %collective-permute-done.5 = f32[8,4,2,2,2,1024]{5,4,3,2,1,0:T(2,128)S(1)} collective-permute-done((f32[8,4,2,2,2,1024]{5,4,3,2,1,0:T(2,128)S(1)}, f32[8,4,2,2,2,1024]{5,4,3,2,1,0:T(2,128)S(1)}, u32[]{:S(2)}, u32[]{:S(2)}) %collective-permute-start.5) | collective-permute-done | bytes 1048608 | tf_op jit(solution)/shard_map/ppermute | solution.py:128
  443.5 22.4 %collective-permute-done.6 = f32[8,4,2,2,2,1024]{5,4,3,2,1,0:T(2,128)S(1)} collective-permute-done((f32[8,4,2,2,2,1024]{5,4,3,2,1,0:T(2,128)S(1)}, f32[8,4,2,2,2,1024]{5,4,3,2,1,0:T(2,128)S(1)}, u32[]{:S(2)}, u32[]{:S(2)}) %collective-permute-start.6) | collective-permute-done | bytes 1048608 | tf_op jit(solution)/shard_map/ppermute | solution.py:128
  468.4 22.5 %collective-permute-done.7 = f32[8,4,2,2,2,1024]{5,4,3,2,1,0:T(2,128)S(1)} collective-permute-done((f32[8,4,2,2,2,1024]{5,4,3,2,1,0:T(2,128)S(1)}, f32[8,4,2,2,2,1024]{5,4,3,2,1,0:T(2,128)S(1)}, u32[]{:S(2)}, u32[]{:S(2)}) %collective-permute-start.7) | collective-permute-done | bytes 1048608 | tf_op jit(solution)/shard_map/ppermute | solution.py:128
  491.9 3.5 collective-permute-start.8
  496.1 43.6 %collective-permute-done.8 = f32[8,4,2,2,2,1024]{5,4,3,2,1,0:T(2,128)S(1)} collective-permute-done((f32[8,4,2,2,2,1024]{5,4,3,2,1,0:T(2,128)S(1)}, f32[8,4,2,2,2,1024]{5,4,3,2,1,0:T(2,128)S(1)}, u32[]{:S(2)}, u32[]{:S(2)}) %collective-permute-start.8) | collective-permute-done | bytes 1048608 | tf_op jit(solution)/shard_map/ppermute | solution.py:128
  (550 shorter events, 186.9 us)
Async XLA Ops:
  7.2 57.2 %copy-start = (f32[8,4,2,2,2,1024]{5,4,3,2,1,0:T(2,128)S(1)}, f32[8,4,2,2,2,1024]{5,4,3,2,1,0:T(2,128)}, u32[]{:S(2)}) copy-start(f32[8,4,2,2,2,1024]{5,4,3,2,1,0:T(2,128)} %param.15) | copy-start | bytes 3145732
  7.2 86.2 %all-reduce.5.cloned.1.call-start = ((), (), s32[]{:S(2)}) async-start(), calls=%async_computation | async-start | bytes 524288 | tf_op jit(solution)/shard_map/psum | solution.py:116
  8.1 13.0 %copy-start.129 = (pred[512]{0:T(512)(128)(4,1)}, pred[512]{0:T(512)(128)(4,1)S(1)}, u32[]{:S(2)}) copy-start(pred[512]{0:T(512)(128)(4,1)S(1)} %compare_and_fusion) | copy-start | bytes 1540
  8.1 29.4 %copy-start.126 = (pred[512]{0:T(512)(128)(4,1)}, pred[512]{0:T(512)(128)(4,1)S(1)}, u32[]{:S(2)}) copy-start(pred[512]{0:T(512)(128)(4,1)S(1)} %compare_and_fusion.1) | copy-start | bytes 1540
  9.4 38.1 %copy-start.6 = (f32[4,2,2,16,512]{4,3,2,1,0:T(8,128)}, f32[4,2,2,16,512]{4,3,2,1,0:T(8,128)S(1)}, u32[]{:S(2)}) copy-start(f32[4,2,2,16,512]{4,3,2,1,0:T(8,128)S(1)} %get-tuple-element.139) | copy-start | bytes 1572868
  9.4 38.1 %copy-start.7 = (f32[4,2,2,16,512]{4,3,2,1,0:T(8,128)}, f32[4,2,2,16,512]{4,3,2,1,0:T(8,128)S(1)}, u32[]{:S(2)}) copy-start(f32[4,2,2,16,512]{4,3,2,1,0:T(8,128)S(1)} %get-tuple-element.140) | copy-start | bytes 1572868
  30.3 10.4 %copy-start.123 = (s32[1024]{0:T(1024)}, s32[1024]{0:T(1024)S(1)}, u32[]{:S(2)}) copy-start(s32[1024]{0:T(1024)S(1)} %pad_clamp_fusion) | copy-start | bytes 12292
  50.1 140.6 %all-reduce.7.cloned.1.call-start = ((), (), s32[]{:S(2)}) async-start(), calls=%async_computation.1 | async-start | bytes 524288 | tf_op jit(solution)/shard_map/psum | solution.py:116
  61.9 31.5 %copy-start.11 = (f32[1,2,2,2,16,512]{5,4,3,2,1,0:T(8,128)S(1)}, f32[1,2,2,2,16,512]{5,4,3,2,1,0:T(8,128)}, u32[]{:S(2)}) copy-start(f32[1,2,2,2,16,512]{5,4,3,2,1,0:T(8,128)} %param.11) | copy-start | bytes 786436
  103.1 12.0 %copy-start.124 = (s32[1024]{0:T(1024)S(1)}, s32[1024]{0:T(1024)}, u32[]{:S(2)}) copy-start(s32[1024]{0:T(1024)} %copy-done.123) | copy-start | bytes 12292
  103.1 19.2 %copy-start.130 = (pred[512]{0:T(512)(128)(4,1)S(1)}, pred[512]{0:T(512)(128)(4,1)}, u32[]{:S(2)}) copy-start(pred[512]{0:T(512)(128)(4,1)} %copy-done.129) | copy-start | bytes 1540
  161.0 201.0 %all-reduce.9.cloned.1.call-start = ((), (), s32[]{:S(2)}) async-start(), calls=%async_computation.2 | async-start | bytes 524288 | tf_op jit(solution)/shard_map/psum | solution.py:116
  169.3 24.0 %collective-permute-start = (f32[8,4,2,2,2,1024]{5,4,3,2,1,0:T(2,128)}, f32[8,4,2,2,2,1024]{5,4,3,2,1,0:T(2,128)}, u32[]{:S(2)}, u32[]{:S(2)}) collective-permute-start(f32[8,4,2,2,2,1024]{5,4,3,2,1,0:T(2,128)} %broadcast_multiply_fusion.2), channel_id=1, source_target_pairs={{0,4},{4,0},{8,12},{12,8},{16,20},{20,16},{24,28},{28,24},{1,5},{5... | collective-permute-start | bytes 3145736 | tf_op jit(solution)/shard_map/ppermute | solution.py:128
  195.4 23.5 %collective-permute-start.1 = (f32[8,4,2,2,2,1024]{5,4,3,2,1,0:T(2,128)S(1)}, f32[8,4,2,2,2,1024]{5,4,3,2,1,0:T(2,128)S(1)}, u32[]{:S(2)}, u32[]{:S(2)}) collective-permute-start(f32[8,4,2,2,2,1024]{5,4,3,2,1,0:T(2,128)S(1)} %fusion.80), channel_id=1, source_target_pairs={{0,8},{4,12},{8,0},{12,4},{16,24},{20,28},{24,16},{28,20},{1,9},{5... | collective-permute-start | bytes 3145736 | tf_op jit(solution)/shard_map/ppermute | solution.py:128
  221.3 46.3 %collective-permute-start.2 = (f32[8,4,2,2,2,1024]{5,4,3,2,1,0:T(2,128)S(1)}, f32[8,4,2,2,2,1024]{5,4,3,2,1,0:T(2,128)S(1)}, u32[]{:S(2)}, u32[]{:S(2)}) collective-permute-start(f32[8,4,2,2,2,1024]{5,4,3,2,1,0:T(2,128)S(1)} %fusion.112), channel_id=1, source_target_pairs={{0,16},{4,20},{8,24},{12,28},{16,0},{20,4},{24,8},{28,12},{1,17},{... | collective-permute-start | bytes 3145736 | tf_op jit(solution)/shard_map/ppermute | solution.py:128
  275.2 58.2 %copy-start.27 = (f32[4,2,2,2,1024]{4,0,3,2,1:T(4,128)}, f32[4,2,2,2,1024]{4,0,3,2,1:T(4,128)S(1)}, u32[]{:S(2)}) copy-start(f32[4,2,2,2,1024]{4,0,3,2,1:T(4,128)S(1)} %get-tuple-element.23) | copy-start | bytes 393220
  275.7 11.5 %copy-start.125 = (s32[1024]{0:T(1024)S(1)}, s32[1024]{0:T(1024)}, u32[]{:S(2)}) copy-start(s32[1024]{0:T(1024)} %copy-done.123) | copy-start | bytes 12292
  275.7 18.7 %copy-start.131 = (pred[512]{0:T(512)(128)(4,1)S(1)}, pred[512]{0:T(512)(128)(4,1)}, u32[]{:S(2)}) copy-start(pred[512]{0:T(512)(128)(4,1)} %copy-done.129) | copy-start | bytes 1540
  335.2 28.1 %collective-permute-start.3 = (f32[8,4,2,2,2,1024]{5,4,3,2,1,0:T(2,128)}, f32[8,4,2,2,2,1024]{5,4,3,2,1,0:T(2,128)S(1)}, u32[]{:S(2)}, u32[]{:S(2)}) collective-permute-start(f32[8,4,2,2,2,1024]{5,4,3,2,1,0:T(2,128)} %broadcast_multiply_fusion.1), channel_id=1, source_target_pairs={{0,4},{4,0},{8,12},{12,8},{16,20},{20,16},{24,28},{28,24},{1,5},{5... | collective-permute-start | bytes 3145736 | tf_op jit(solution)/shard_map/ppermute | solution.py:128
  364.1 23.7 %collective-permute-start.4 = (f32[8,4,2,2,2,1024]{5,4,3,2,1,0:T(2,128)S(1)}, f32[8,4,2,2,2,1024]{5,4,3,2,1,0:T(2,128)S(1)}, u32[]{:S(2)}, u32[]{:S(2)}) collective-permute-start(f32[8,4,2,2,2,1024]{5,4,3,2,1,0:T(2,128)S(1)} %fusion.81), channel_id=1, source_target_pairs={{0,8},{4,12},{8,0},{12,4},{16,24},{20,28},{24,16},{28,20},{1,9},{5... | collective-permute-start | bytes 3145736 | tf_op jit(solution)/shard_map/ppermute | solution.py:128
  388.9 46.5 %collective-permute-start.5 = (f32[8,4,2,2,2,1024]{5,4,3,2,1,0:T(2,128)S(1)}, f32[8,4,2,2,2,1024]{5,4,3,2,1,0:T(2,128)S(1)}, u32[]{:S(2)}, u32[]{:S(2)}) collective-permute-start(f32[8,4,2,2,2,1024]{5,4,3,2,1,0:T(2,128)S(1)} %fusion.111), channel_id=1, source_target_pairs={{0,16},{4,20},{8,24},{12,28},{16,0},{20,4},{24,8},{28,12},{1,17},{... | collective-permute-start | bytes 3145736 | tf_op jit(solution)/shard_map/ppermute | solution.py:128
  441.7 24.2 %collective-permute-start.6 = (f32[8,4,2,2,2,1024]{5,4,3,2,1,0:T(2,128)S(1)}, f32[8,4,2,2,2,1024]{5,4,3,2,1,0:T(2,128)S(1)}, u32[]{:S(2)}, u32[]{:S(2)}) collective-permute-start(f32[8,4,2,2,2,1024]{5,4,3,2,1,0:T(2,128)S(1)} %broadcast_multiply_fusion), channel_id=1, source_target_pairs={{0,4},{4,0},{8,12},{12,8},{16,20},{20,16},{24,28},{28,24},{1,5},{5... | collective-permute-start | bytes 3145736 | tf_op jit(solution)/shard_map/ppermute | solution.py:128
  466.6 24.2 %collective-permute-start.7 = (f32[8,4,2,2,2,1024]{5,4,3,2,1,0:T(2,128)S(1)}, f32[8,4,2,2,2,1024]{5,4,3,2,1,0:T(2,128)S(1)}, u32[]{:S(2)}, u32[]{:S(2)}) collective-permute-start(f32[8,4,2,2,2,1024]{5,4,3,2,1,0:T(2,128)S(1)} %fusion.82), channel_id=1, source_target_pairs={{0,8},{4,12},{8,0},{12,4},{16,24},{20,28},{24,16},{28,20},{1,9},{5... | collective-permute-start | bytes 3145736 | tf_op jit(solution)/shard_map/ppermute | solution.py:128
  491.9 47.8 %collective-permute-start.8 = (f32[8,4,2,2,2,1024]{5,4,3,2,1,0:T(2,128)S(1)}, f32[8,4,2,2,2,1024]{5,4,3,2,1,0:T(2,128)S(1)}, u32[]{:S(2)}, u32[]{:S(2)}) collective-permute-start(f32[8,4,2,2,2,1024]{5,4,3,2,1,0:T(2,128)S(1)} %fusion.110), channel_id=1, source_target_pairs={{0,16},{4,20},{8,24},{12,28},{16,0},{20,4},{24,8},{28,12},{1,17},{... | collective-permute-start | bytes 3145736 | tf_op jit(solution)/shard_map/ppermute | solution.py:128
  (123 other events, 340.2 us)
Sparse Core Ops, SparseCore 0:
  50.2 35.0 all-reduce.4
  161.1 29.5 all-reduce.6
  328.3 33.6 all-reduce.8
